TPU v7x, 512 devices: a whole 4x8x8 slice. The times are simulated.
512 devices in a mesh: row: 16 (over z, core), col: 32 (over y, x).
Axes of the slice: x: 4, y: 8, z: 8, core: 2. Of those that a mesh axis runs over, the one named last changes fastest.
Arguments:
- air_flux: bfloat16 [4, 65536, 16, 128], P(None, ('row', 'col')), may hold values from -1 to 3
- air_area: float32 [65536, 128], P(('row', 'col')), may hold values from 0.2 to 2
- sea_area: float32 [65536, 128], P(('row', 'col')), may hold values from 0.2 to 2
- wet_mask: int32 [65536], P(('row', 'col')), may hold values 0 or 1
- intersection_tiles: bfloat16 [32, 128, 128], replicated, may hold values from -0.125 to 0.125
- send_block: int32 [512, 256], P(('row', 'col')), may hold values from 0 to 127
- target_slot: int32 [65536, 16], P(('row', 'col')), may hold values from 0 to 255
- target_tile: int32 [65536, 16], P(('row', 'col')), may hold values from 0 to 31, as said below
Outputs:
- sea_flux: float32 [65536, 16, 128], P(('row', 'col'))
Inputs may be any that keep to these rules, and one draw needn't show every extreme that they name: `target_tile`: the 16 entries of a row are distinct.
All inputs are finite; a program needn't handle non-finite values. No bound on the sum of `wet_mask` on one device may be relied on, other than what follows from the above.
Results may differ from a plain program's by a relative error of at most 0.0003.
The roundings to bfloat16 on the way count: a program that leaves them out, or rounds other values in their place, can miss the bound.
Values may be sent and summed in bfloat16 or wider, within the bound.
A program may use at most 128 MiB of HBM per device.

v0:
```python
import jax
import jax.numpy as jnp
from jax import lax
from jax.sharding import Mesh
from jax.sharding import PartitionSpec as P

NSTEPS = 4
COL = ("col_0", "col_1")
ROW_COL = ("row_0", "row_1", "col_0", "col_1")


def by_axis(array, axes):
    for axis in axes:
        array = lax.psum(array, axis)
    return array


def regrid_fields(source_rows, row_index, tile_index, intersection_tiles):
    targets = tile_index.shape[0]
    intersections = tile_index.shape[1]
    fields = source_rows.shape[1]
    cell_count = source_rows.shape[2]
    picked = jnp.take(source_rows, row_index.reshape(-1), axis=0).reshape(
        targets, intersections, fields, cell_count
    )
    tile_ids = jnp.arange(intersection_tiles.shape[0], dtype=jnp.int32)
    onehot = (tile_index[:, :, None] == tile_ids[None, None, :]).astype(jnp.bfloat16)
    grouped = jnp.einsum(
        "tkw,tkfc->twfc", onehot, picked, preferred_element_type=jnp.float32
    ).astype(jnp.bfloat16)
    return jnp.einsum(
        "twfc,wcd->tfd", grouped, intersection_tiles, preferred_element_type=jnp.float32
    )


def body(
    air_flux, air_area, sea_area, wet_mask, intersection_tiles, send_block, target_slot, target_tile
):
    mean_flux = jnp.sum(air_flux, axis=0, dtype=jnp.float32) / NSTEPS
    sent_flux = mean_flux.astype(jnp.bfloat16)
    air_part = jnp.sum(mean_flux * air_area[:, None, :], axis=(0, 2))
    outbound = jnp.take(sent_flux, send_block[0], axis=0)
    raw_flux = regrid_fields(
        lax.all_to_all(outbound, COL, split_axis=0, concat_axis=0, tiled=True),
        target_slot,
        target_tile,
        intersection_tiles,
    )
    wet_float = wet_mask.astype(jnp.float32)
    wet_area = wet_float[:, None] * sea_area
    sea_part = jnp.sum(raw_flux * wet_area[:, None, :], axis=(0, 2))
    wet_part = jnp.sum(wet_area)
    air_total, sea_total, wet_sum = (
        by_axis(air_part, ROW_COL),
        by_axis(sea_part, ROW_COL),
        by_axis(wet_part, ROW_COL),
    )
    shift = (air_total - sea_total) / jnp.maximum(wet_sum, 1.0)
    return wet_float[:, None, None] * (raw_flux + shift[None, :, None])


def solution(mesh):
    torus = Mesh(mesh.devices.reshape(8, 2, 8, 4), ("row_0", "row_1", "col_0", "col_1"))
    return jax.shard_map(
        body,
        mesh=torus,
        in_specs=(
            P(None, ROW_COL, None, None),
            P(ROW_COL, None),
            P(ROW_COL, None),
            P(ROW_COL),
            P(),
            P(ROW_COL, None),
            P(ROW_COL, None),
            P(ROW_COL, None),
        ),
        out_specs=P(ROW_COL, None, None),
        check_vma=False,
    )
```

profile of v0, /device:TPU:8, one launch (start us, length us, event | category | flops | bytes accessed | tf_op | source)
XLA Modules:
  0.0 147.2 jit_solution(10666747091214727924)
XLA Ops:
  0.0 0.0 copy-start
  0.0 0.0 copy-start.4
  0.0 0.0 copy-start.2
  0.0 0.0 copy-start.3
  0.0 0.0 copy-start.1
  0.0 0.8 compare_select_fusion.2
  0.8 0.7 compare_and_fusion.1
  1.5 0.8 broadcast_multiply_fusion.1
  2.3 2.0 %convert_reduce_fusion = f32[128,16,128]{2,1,0:T(8,128)S(1)} fusion(bf16[4,128,16,128]{3,2,1,0:T(8,128)(2,1)} %param.8), kind=kLoop, calls=%fused_computation.8 | loop fusion | flops 1835008 | bytes 3145728 | tf_op jit(solution)/shard_map/reduce_sum | solution.py:39
  4.4 0.3 multiply_reduce_fusion.1
  4.7 0.8 gather_fusion
  5.5 1.7 %broadcast_select_fusion = bf16[256,16,128]{2,1,0:T(8,128)(2,1)} fusion(bf16[256,16,128]{2,1,0:T(8,128)(2,1)S(1)} %gather_fusion, pred[256]{0:T(512)(128)(4,1)S(1)} %compare_and_fusion.1), kind=kLoop, calls=%fused_computation.16 | loop fusion | flops 524288 | bytes 2097408 | tf_op jit(solution)/shard_map/jit(_take)/select_n | solution.py:42
  7.3 10.2 %all-to-all-start = ((bf16[256,16,128]{2,1,0:T(8,128)(2,1)}), bf16[256,16,128]{2,1,0:T(8,128)(2,1)S(1)}, u32[]{:S(2)}, u32[]{:S(2)}) async-start(bf16[256,16,128]{2,1,0:T(8,128)(2,1)} %broadcast_select_fusion), calls=%async_computation | async-start | bytes 2097152 | tf_op jit(solution)/shard_map/all_to_all | solution.py:44
  17.4 0.0 copy-done.4
  17.4 0.0 copy-done.2
  17.5 0.1 copy.18
  17.6 0.1 copy.17
  17.7 0.0 copy-done.3
  17.7 0.1 copy.16
  17.8 0.1 reshape.80
  17.9 0.0 copy-done.1
  17.9 0.7 fusion.12
  18.6 26.0 %all-to-all-done = bf16[256,16,128]{2,1,0:T(8,128)(2,1)S(1)} async-done(((bf16[256,16,128]{2,1,0:T(8,128)(2,1)}), bf16[256,16,128]{2,1,0:T(8,128)(2,1)S(1)}, u32[]{:S(2)}, u32[]{:S(2)}) %all-to-all-start) | async-done | bytes 1048608 | tf_op jit(solution)/shard_map/all_to_all | solution.py:44
  44.6 16.3 %gather_fusion.1 = bf16[2048,16,128]{2,1,0:T(8,128)(2,1)} fusion(bf16[256,16,128]{2,1,0:T(8,128)(2,1)S(1)} %all-to-all-done, s32[2048]{0:T(1024)S(1)} %broadcast_clamp_fusion), kind=kCustom, calls=%fused_computation.1 | custom fusion | bytes 16785408 | tf_op jit(solution)/shard_map/jit(_take)/gather | solution.py:23
  60.9 12.9 %convolution_convert_fusion = bf16[128,32,16,128]{3,1,2,0:T(8,128)(2,1)} fusion(bf16[128,16,16,128]{3,2,1,0:T(8,128)(2,1)} %bitcast.19, pred[128,16]{1,0:T(8,128)(4,1)S(1)} %copy.17, s32[128,16]{1,0:T(8,128)S(1)} %copy.16), kind=kOutput, calls=%fused_computation.4 | convolution fusion | flops 281083904 | bytes 25176064 | tf_op jit(solution)/shard_map/tkw,tkfc->twfc/dot_general | solution.py:28
  73.8 0.0 copy-done
  73.8 16.8 %multiply_reduce_fusion = (f32[16]{0:T(128)S(1)}, f32[128,16,128]{2,0,1:T(8,128)S(1)}) fusion(f32[128,128]{1,0:T(8,128)S(1)} %get-tuple-element.18, bf16[32,128,128]{2,1,0:T(8,128)(2,1)S(1)} %copy-done, bf16[128,32,16,128]{3,1,2,0:T(8,128)(2,1)} %convolution_convert_fusion), kind=kOutput, calls=%fused_computation.12 | convolution fusion | flops 2148007936 | bytes 18939968 | tf_op jit(solution)/shard_map/twfc,wcd->tfd/dot_general | solution.py:31
  90.6 23.8 %all-reduce.1 = (f32[16]{0:T(128)S(1)}, f32[16]{0:T(128)S(1)}, f32[]{:T(128)}) all-reduce(f32[16]{0:T(128)S(1)} %get-tuple-element.19, f32[16]{0:T(128)S(1)} %get-tuple-element.21, f32[]{:T(128)} %get-tuple-element.17), channel_id=1, replica_groups=mesh['row_0'=8,'row_1'=2,'col_0'=8,'col_1'=4] {'row_0'}, use_global_device_ids=true, to_apply=%region_2.3 | all-reduce | flops 33 | bytes 264 | tf_op jit(solution)/shard_map/psum | solution.py:14
  114.4 3.1 %all-reduce.3 = (f32[16]{0:T(128)S(1)}, f32[16]{0:T(128)S(1)}, f32[]{:T(128)}) all-reduce(f32[16]{0:T(128)S(1)} %get-tuple-element.8, f32[16]{0:T(128)S(1)} %get-tuple-element.9, f32[]{:T(128)} %get-tuple-element.10), channel_id=1, replica_groups=mesh['row_0'=8,'row_1'=2,'col_0'=8,'col_1'=4] {'row_1'}, use_global_device_ids=true, to_apply=%region_3.4 | all-reduce | flops 33 | bytes 264 | tf_op jit(solution)/shard_map/psum | solution.py:14
  117.5 16.0 %all-reduce = (f32[16]{0:T(128)S(1)}, f32[16]{0:T(128)S(1)}, f32[]{:T(128)}) all-reduce(f32[16]{0:T(128)S(1)} %get-tuple-element.14, f32[16]{0:T(128)S(1)} %get-tuple-element.15, f32[]{:T(128)} %get-tuple-element.16), channel_id=1, replica_groups=mesh['row_0'=8,'row_1'=2,'col_0'=8,'col_1'=4] {'col_0'}, use_global_device_ids=true, to_apply=%region_4.5 | all-reduce | flops 33 | bytes 264 | tf_op jit(solution)/shard_map/psum | solution.py:14
  133.5 11.2 %all-reduce.2 = (f32[16]{0:T(128)S(1)}, f32[16]{0:T(128)S(1)}, f32[]{:T(128)}) all-reduce(f32[16]{0:T(128)S(1)} %get-tuple-element.5, f32[16]{0:T(128)S(1)} %get-tuple-element.6, f32[]{:T(128)} %get-tuple-element.7), channel_id=1, replica_groups=mesh['row_0'=8,'row_1'=2,'col_0'=8,'col_1'=4] {'col_1'}, use_global_device_ids=true, to_apply=%region_5.6 | all-reduce | flops 33 | bytes 264 | tf_op jit(solution)/shard_map/psum | solution.py:14
  145.4 0.2 add_multiply_fusion
  145.6 1.6 %copy.21 = f32[128,16,128]{2,1,0:T(8,128)} copy(f32[128,16,128]{2,0,1:T(8,128)S(1)} %add_multiply_fusion) | data formatting | bytes 2097152 | tf_op jit(solution)/shard_map/mul | solution.py:59
  (6 shorter events, 0.0 us)
Async XLA Ops:
  0.0 73.8 %copy-start = (bf16[32,128,128]{2,1,0:T(8,128)(2,1)S(1)}, bf16[32,128,128]{2,1,0:T(8,128)(2,1)}, u32[]{:S(2)}) copy-start(bf16[32,128,128]{2,1,0:T(8,128)(2,1)} %param.12) | copy-start | bytes 3145732
  0.0 17.4 %copy-start.4 = (s32[128]{0:T(128)S(1)}, s32[128]{0:T(128)}, u32[]{:S(2)}) copy-start(s32[128]{0:T(128)} %param.11) | copy-start | bytes 1540
  0.0 17.4 %copy-start.2 = (s32[128,16]{0,1:T(8,128)S(1)}, s32[128,16]{0,1:T(8,128)}, u32[]{:S(2)}) copy-start(s32[128,16]{0,1:T(8,128)} %param.14) | copy-start | bytes 24580
  0.0 17.7 %copy-start.3 = (s32[128,16]{0,1:T(8,128)S(1)}, s32[128,16]{0,1:T(8,128)}, u32[]{:S(2)}) copy-start(s32[128,16]{0,1:T(8,128)} %param.15) | copy-start | bytes 24580
  0.0 17.9 %copy-start.1 = (f32[128,128]{1,0:T(8,128)S(1)}, f32[128,128]{1,0:T(8,128)}, u32[]{:S(2)}) copy-start(f32[128,128]{1,0:T(8,128)} %param.10) | copy-start | bytes 196612
  7.3 37.3 %all-to-all-start = ((bf16[256,16,128]{2,1,0:T(8,128)(2,1)}), bf16[256,16,128]{2,1,0:T(8,128)(2,1)S(1)}, u32[]{:S(2)}, u32[]{:S(2)}) async-start(bf16[256,16,128]{2,1,0:T(8,128)(2,1)} %broadcast_select_fusion), calls=%async_computation | async-start | bytes 2097152 | tf_op jit(solution)/shard_map/all_to_all | solution.py:44
where the time goes:
time: 148 us; the launch traced here: 147 us
  blocking collectives  54.1 us (37%)
  matrix products  29.7 us (20%)
  waiting for transfers between devices  26 us (18%)
  local copies, waits for them, and re-layouts  19.1 us (13%)
  starting transfers between devices  10.2 us (7%)
  other arithmetic  7.32 us (5%)
    psum x4, blocking collectives, by_axis(): array = lax.psum(array, axis)  54.1 us
    all_to_all x1, waiting for transfers between devices, body(): lax.all_to_all(outbound, COL, split_axis=0, concat_axis=0, tiled=True)  26 us
    dot_general x1, matrix products, regrid_fields(): jnp.einsum('twfc,wcd->tfd', grouped, intersection_tiles, preferred_elemen...  16.8 us
    gather x1, local copies, waits for them, and re-layouts, regrid_fields(): jnp.take(source_rows, row_index.reshape(-1), axis=0)  16.3 us
    dot_general x1, matrix products, regrid_fields(): jnp.einsum('tkw,tkfc->twfc', onehot, picked, preferred_element_type=jnp.f...  12.9 us
    all_to_all x1, starting transfers between devices, body(): lax.all_to_all(outbound, COL, split_axis=0, concat_axis=0, tiled=True)  10.2 us
  transfers between devices with their start and end apart: 1, of which 1 were waited for; matrix products, arithmetic and copies ran while one was open for 1% of the time, Pallas kernels for 0%

commit v1 on v0

v1 whole, which is shorter than its diff:
```python
import functools

import jax
import jax.numpy as jnp
from jax import lax
from jax.experimental import pallas as pl
from jax.experimental.pallas import tpu as pltpu
from jax.sharding import PartitionSpec as P

MESH = pl.DeviceIdType.MESH
WIDE = ("row", "col")
CHUNKS = 4


def peer_order(n_col):
    ny, nx = (8, 4) if n_col == 32 else (n_col, 1)
    ys = sorted(range(ny), key=lambda d: (-min(d, ny - d), d))
    return ny, nx, [(dy, dx) for dx in range(nx) for dy in ys if (dy, dx) != (0, 0)]


def kernel(
    n_row, n_col,
    send_ref, inverse_ref, air_ref, air_area_ref, sea_area_ref, wet_ref, tiles_ref,
    raw_ref, shift_ref,
    air, sent, outbound, received, grouped, part, rows, part_all, cols,
    load_sem, send_sem, recv_sem, row_send, row_recv, col_send, col_recv,
):
    steps, blocks, fields, cells = air.shape
    cap = outbound.shape[0] // n_col
    slots = n_col * cap
    ntiles = tiles_ref.shape[0] // cells
    ny, nx, order = peer_order(n_col)
    me_row = lax.axis_index("row")
    me_col = lax.axis_index("col")
    per = blocks // CHUNKS

    def load(chunk):
        at = pl.ds(chunk * per, per)
        return pltpu.make_async_copy(air_ref.at[:, at], air.at[:, at], load_sem.at[chunk])

    for chunk in range(CHUNKS):
        load(chunk).start()
    barrier = pltpu.get_barrier_semaphore()
    for step in range(1, n_col):
        pl.semaphore_signal(
            barrier, inc=1, device_id={"col": lax.rem(me_col + step, n_col)}, device_id_type=MESH
        )
    for step in range(1, n_row):
        pl.semaphore_signal(
            barrier, inc=1, device_id={"row": lax.rem(me_row + step, n_row)}, device_id_type=MESH
        )

    acc = jnp.zeros((fields, cells), jnp.float32)
    for chunk in range(CHUNKS):
        load(chunk).wait()

        def average(b, acc):
            total = air[0, b].astype(jnp.float32)
            for step in range(1, steps):
                total = total + air[step, b].astype(jnp.float32)
            mean = total * (1.0 / steps)
            sent[b] = mean.astype(jnp.bfloat16)
            return acc + mean * air_area_ref[pl.ds(b, 1), :]

        acc = lax.fori_loop(chunk * per, (chunk + 1) * per, average, acc, unroll=8)

    received[slots] = jnp.zeros((fields, cells), jnp.bfloat16)
    mine = me_col * cap
    pl.semaphore_wait(barrier, n_col + n_row - 2)

    me_y, me_x = me_col // nx, lax.rem(me_col, nx)
    for dy, dx in order:
        peer = lax.rem(me_y + dy, ny) * nx + lax.rem(me_x + dx, nx)
        for j in range(cap):
            outbound[peer * cap + j] = sent[send_ref[0, peer * cap + j]]
        pltpu.make_async_remote_copy(
            src_ref=outbound.at[pl.ds(peer * cap, cap)],
            dst_ref=received.at[pl.ds(mine, cap)],
            send_sem=send_sem,
            recv_sem=recv_sem,
            device_id={"col": peer},
            device_id_type=MESH,
        ).start()
    for j in range(cap):
        received[mine + j] = sent[send_ref[0, mine + j]]

    whole = received.at[pl.ds(0, slots - cap)]
    pltpu.make_async_copy(whole, whole, recv_sem).wait()

    chunk_targets = grouped.shape[0] // fields
    targets = blocks

    def regrid(chunk, sea):
        base = chunk * chunk_targets
        for t in range(chunk_targets):
            for w in range(ntiles):
                slot = inverse_ref[(base + t) * ntiles + w]
                grouped[t * fields:(t + 1) * fields, w * cells:(w + 1) * cells] = received[slot]
        raw = jnp.dot(grouped[...], tiles_ref[...], preferred_element_type=jnp.float32)
        raw = raw.reshape(chunk_targets, fields, cells)
        raw_ref[pl.ds(pl.multiple_of(base, chunk_targets), chunk_targets)] = raw
        at = pl.ds(pl.multiple_of(base, chunk_targets), chunk_targets)
        area = sea_area_ref[at, :] * wet_ref[at, :]
        return sea + jnp.sum(raw * area[:, None, :], axis=0)

    acc = acc - lax.fori_loop(
        0, targets // chunk_targets, regrid, jnp.zeros((fields, cells), jnp.float32)
    )

    lane = lax.broadcasted_iota(jnp.int32, (fields, cells), 1)
    field = lax.broadcasted_iota(jnp.int32, (fields, cells), 0)
    diff = jnp.sum(acc, axis=1, keepdims=True)
    line = jnp.sum(jnp.where(lane == field, diff, 0.0), axis=0, keepdims=True)
    wet = jnp.sum(sea_area_ref[...] * wet_ref[...], axis=0, keepdims=True)
    wet = jnp.sum(wet, axis=1, keepdims=True)
    line = line + jnp.where(lane[:1] == fields, wet, 0.0)

    def gather_sum(line, part, into, n, me, axis, s_sem, r_sem):
        part[0] = line
        into[me] = line
        for step in range(1, n):
            pltpu.make_async_remote_copy(
                src_ref=part.at[0],
                dst_ref=into.at[me],
                send_sem=s_sem,
                recv_sem=r_sem,
                device_id={axis: lax.rem(me + step, n)},
                device_id_type=MESH,
            ).start()
        others = into.at[pl.ds(0, n - 1)]
        pltpu.make_async_copy(others, others, r_sem).wait()
        return jnp.sum(into[...], axis=0)

    line = gather_sum(line, part, rows, n_row, me_row, "row", row_send, row_recv)
    line = gather_sum(line, part_all, cols, n_col, me_col, "col", col_send, col_recv)
    line = jnp.broadcast_to(line, (fields, cells))
    diff = jnp.sum(jnp.where(lane == field, line, 0.0), axis=1, keepdims=True)
    wet = jnp.sum(jnp.where(lane == fields, line, 0.0), axis=1, keepdims=True)
    shift_ref[...] = jnp.broadcast_to(diff / jnp.maximum(wet, 1.0), (fields, cells))

    pltpu.make_async_copy(whole, whole, send_sem).wait()
    others = rows.at[pl.ds(0, n_row - 1)]
    pltpu.make_async_copy(others, others, row_send).wait()
    others = cols.at[pl.ds(0, n_col - 1)]
    pltpu.make_async_copy(others, others, col_send).wait()


def body(n_row, n_col, air_flux, air_area, sea_area, wet_mask, tiles, send_block, slot, tile):
    steps, blocks, fields, cells = air_flux.shape
    ntiles = tiles.shape[0]
    slots = send_block.shape[1]
    ids = jnp.arange(ntiles, dtype=jnp.int32)
    inverse = slots + jnp.sum(
        jnp.where(tile[:, :, None] == ids, slot[:, :, None] - slots, 0), axis=1, dtype=jnp.int32
    )
    wet = wet_mask.astype(jnp.float32)
    wet_wide = jnp.broadcast_to(wet[:, None], (blocks, cells))
    vmem = pl.BlockSpec(memory_space=pltpu.VMEM)
    smem = pl.BlockSpec(memory_space=pltpu.SMEM)
    raw, shift = pl.pallas_call(
        functools.partial(kernel, n_row, n_col),
        out_shape=(
            jax.ShapeDtypeStruct((blocks, fields, cells), jnp.float32),
            jax.ShapeDtypeStruct((fields, cells), jnp.float32),
        ),
        in_specs=[smem, smem, pl.BlockSpec(memory_space=pltpu.HBM), vmem, vmem, vmem, vmem],
        out_specs=(vmem, vmem),
        scratch_shapes=[
            pltpu.VMEM((steps, blocks, fields, cells), jnp.bfloat16),
            pltpu.VMEM((blocks, fields, cells), jnp.bfloat16),
            pltpu.VMEM((slots, fields, cells), jnp.bfloat16),
            pltpu.VMEM((slots + 1, fields, cells), jnp.bfloat16),
            pltpu.VMEM((32 * fields, ntiles * cells), jnp.bfloat16),
            pltpu.VMEM((1, 1, cells), jnp.float32),
            pltpu.VMEM((n_row, 1, cells), jnp.float32),
            pltpu.VMEM((1, 1, cells), jnp.float32),
            pltpu.VMEM((n_col, 1, cells), jnp.float32),
            pltpu.SemaphoreType.DMA((CHUNKS,)),
        ] + [pltpu.SemaphoreType.DMA] * 6,
        compiler_params=pltpu.CompilerParams(
            collective_id=0, has_side_effects=True, vmem_limit_bytes=60 * 1024 * 1024
        ),
    )(
        send_block, inverse.reshape(-1), air_flux, air_area, sea_area, wet_wide,
        tiles.reshape(ntiles * cells, cells),
    )
    return wet[:, None, None] * (raw + shift[None])


def solution(mesh):
    n_row, n_col = mesh.shape["row"], mesh.shape["col"]
    return jax.shard_map(
        functools.partial(body, n_row, n_col),
        mesh=mesh,
        in_specs=(
            P(None, WIDE, None, None), P(WIDE, None), P(WIDE, None), P(WIDE), P(),
            P(WIDE, None), P(WIDE, None), P(WIDE, None),
        ),
        out_specs=P(WIDE, None, None),
        check_vma=False,
    )
```

time: 148 us -> 67.7 us (0.46)
  the two profiles are of different devices: /device:TPU:8 before, /device:TPU:1 now
where the time goes in v1:
time: 67.7 us; the launch traced here: 67.4 us
  Pallas kernels  61.4 us (91%)
  other arithmetic  4.5 us (7%)
  local copies, waits for them, and re-layouts  1.49 us (2%)
    pallas_call x1, Pallas kernels, body(): pl.pallas_call(functools.partial(kernel, n_row, n_col), out_shape=(jax.Sh...  61.4 us
    mul x1, other arithmetic, body(): return wet[:, None, None] * (raw + shift[None])  2.4 us

profile of v1, /device:TPU:1, one launch (start us, length us, event | category | flops | bytes accessed | tf_op | source)
XLA Modules:
  0.0 67.4 jit_solution(11886964387059160285)
XLA Ops:
  0.0 0.7 convert_element_type.3
  0.7 0.7 %broadcast_add_fusion.1 = s32[128,16]{0,1:T(8,128)S(1)} fusion(s32[128,16]{0,1:T(8,128)} %param.14), kind=kLoop, calls=%fused_computation.4 | loop fusion | flops 2048 | bytes 16384 | tf_op jit(solution)/shard_map/sub | solution.py:154
  1.4 0.7 %select_reduce_fusion = s32[128,32]{0,1:T(8,128)S(1)} fusion(s32[128,16]{0,1:T(8,128)S(1)} %broadcast_add_fusion.1, s32[128,16]{0,1:T(8,128)} %param.15), kind=kLoop, calls=%fused_computation.1 | loop fusion | flops 192512 | bytes 32768 | tf_op jit(solution)/shard_map/reduce_sum | solution.py:153
  2.1 0.1 copy.13
  2.2 0.7 %add.22.inverse_ref = s32[4096]{0:T(1024)} reshape(s32[128,32]{1,0:T(8,128)S(1)} %copy.13) | data formatting | bytes 32768 | tf_op jit(solution)/shard_map/add | solution.py:153
  2.9 0.7 %broadcast_in_dim.16.wet_ref = f32[128,128]{1,0:T(8,128)} broadcast(f32[128]{0:T(128)S(1)} %convert_element_type.3), dimensions={0} | broadcast | bytes 66048 | tf_op jit(solution)/shard_map/broadcast_in_dim | solution.py:157
  3.6 61.4 %shard_map.82 = (f32[128,16,128]{2,1,0:T(8,128)}, f32[16,128]{1,0:T(8,128)}) custom-call(s32[1,256]{1,0:T(1,128)} %send_ref.1, s32[4096]{0:T(1024)} %add.22.inverse_ref, bf16[4,128,16,128]{3,2,1,0:T(8,128)(2,1)} %air_ref.1, f32[128,128]{1,0:T(8,128)} %air_area_ref.1, f32[128,128]{1,0:T(8,128)} %sea_area_ref.1, f32[128,128]{1,0:T(8,128)} %broadcast_in_dim.16.wet_ref, ...), custom_call_target="tpu_custom_call" | custom-call | tf_op jit(solution)/shard_map/pallas_call | solution.py:160
  65.0 2.4 %add_multiply_fusion = f32[128,16,128]{2,1,0:T(8,128)} fusion(f32[128,16,128]{2,1,0:T(8,128)} %get-tuple-element.7, f32[16,128]{1,0:T(8,128)} %get-tuple-element.8, f32[128]{0:T(128)S(1)} %convert_element_type.3), kind=kLoop, calls=%fused_computation | loop fusion | flops 524288 | bytes 2105856 | tf_op jit(solution)/shard_map/mul | solution.py:187
  (1 shorter events, 0.0 us)

commit v2 on v1

v2 whole, which is shorter than its diff:
```python
import functools

import jax
import jax.numpy as jnp
from jax import lax
from jax.experimental import pallas as pl
from jax.experimental.pallas import tpu as pltpu
from jax.sharding import PartitionSpec as P

MESH = pl.DeviceIdType.MESH
WIDE = ("row", "col")
CHUNKS = 4


def peer_order(n_col):
    ny, nx = (8, 4) if n_col == 32 else (n_col, 1)
    ys = sorted(range(ny), key=lambda d: (-min(d, ny - d), d))
    return ny, nx, [(dy, dx) for dx in range(nx) for dy in ys if (dy, dx) != (0, 0)][::-1]


def three_parts(x):
    high = x.astype(jnp.bfloat16)
    rest = x - high.astype(jnp.float32)
    middle = rest.astype(jnp.bfloat16)
    low = (rest - middle.astype(jnp.float32)).astype(jnp.bfloat16)
    return high, middle, low


def kernel(
    n_row, n_col,
    send_ref, slot_ref, tile_ref, air_ref, air_area_ref, sea_area_ref, wet_ref, tiles_ref,
    raw_ref, shift_ref,
    send, slot_of, tile_of, air, air_area, sea_area, wet, tiles,
    inverse_v, inverse, sent, outbound, received, grouped, adjoint, part, rows, part_all, cols,
    small_sem, load_sem, inverse_sem, send_sem, recv_sem, row_send, row_recv, col_send, col_recv,
):
    steps, blocks, fields, cells = air.shape
    cap = outbound.shape[0] // n_col
    slots = n_col * cap
    ntiles = tiles.shape[0]
    ny, nx, order = peer_order(n_col)
    me_row = lax.axis_index("row")
    me_col = lax.axis_index("col")
    per = blocks // CHUNKS

    small = [
        pltpu.make_async_copy(source, target, small_sem.at[i])
        for i, (source, target) in enumerate((
            (send_ref, send), (air_area_ref, air_area), (slot_ref, slot_of), (tile_ref, tile_of),
            (wet_ref, wet), (sea_area_ref, sea_area), (tiles_ref, tiles),
        ))
    ]

    def load(chunk):
        at = pl.ds(chunk * per, per)
        return pltpu.make_async_copy(air_ref.at[:, at], air.at[:, at], load_sem.at[chunk])

    for copy in small[:2]:
        copy.start()
    for chunk in range(CHUNKS):
        load(chunk).start()
    for copy in small[2:]:
        copy.start()
    barrier = pltpu.get_barrier_semaphore()
    for step in range(1, n_col):
        pl.semaphore_signal(
            barrier, inc=1, device_id={"col": lax.rem(me_col + step, n_col)}, device_id_type=MESH
        )
    for step in range(1, n_row):
        pl.semaphore_signal(
            barrier, inc=1, device_id={"row": lax.rem(me_row + step, n_row)}, device_id_type=MESH
        )

    acc = jnp.zeros((fields, cells), jnp.float32)
    for copy in small[:2]:
        copy.wait()
    for chunk in range(CHUNKS):
        load(chunk).wait()

        def average(b, acc):
            total = air[0, b].astype(jnp.float32)
            for step in range(1, steps):
                total = total + air[step, b].astype(jnp.float32)
            mean = total * (1.0 / steps)
            sent[b] = mean.astype(jnp.bfloat16)
            return acc + mean * air_area[pl.ds(b, 1), :]

        acc = lax.fori_loop(chunk * per, (chunk + 1) * per, average, acc, unroll=4)

    for copy in small[2:4]:
        copy.wait()
    tile_id = lax.broadcasted_iota(jnp.int32, (ntiles, blocks), 0)
    found = jnp.full((ntiles, blocks), slots, jnp.int32)
    for k in range(slot_of.shape[0]):
        found = jnp.where(tile_of[k:k + 1, :] == tile_id, slot_of[k:k + 1, :], found)
    inverse_v[...] = found
    received[slots] = jnp.zeros((fields, cells), jnp.bfloat16)
    mine = me_col * cap
    pl.semaphore_wait(barrier, n_col + n_row - 2)

    me_y, me_x = me_col // nx, lax.rem(me_col, nx)
    for i, (dy, dx) in enumerate(order):
        peer = lax.rem(me_y + dy, ny) * nx + lax.rem(me_x + dx, nx)
        for j in range(cap):
            outbound[peer * cap + j] = sent[send[0, peer * cap + j]]
        pltpu.make_async_remote_copy(
            src_ref=outbound.at[pl.ds(peer * cap, cap)],
            dst_ref=received.at[pl.ds(mine, cap)],
            send_sem=send_sem,
            recv_sem=recv_sem.at[i],
            device_id={"col": peer},
            device_id_type=MESH,
        ).start()
    for j in range(cap):
        received[mine + j] = sent[send[0, mine + j]]
    to_scalars = pltpu.make_async_copy(inverse_v, inverse, inverse_sem)
    to_scalars.start()

    for copy in small[4:]:
        copy.wait()
    square = (blocks, blocks)
    on_diagonal = (
        lax.broadcasted_iota(jnp.int32, square, 0) == lax.broadcasted_iota(jnp.int32, square, 1)
    )
    wet_wide = jnp.broadcast_to(wet[...].astype(jnp.float32), square)
    wet_column = jnp.sum(jnp.where(on_diagonal, wet_wide, 0.0), axis=1, keepdims=True)
    wet_area = sea_area[...] * wet_column
    wet_sum = jnp.sum(jnp.sum(wet_area, axis=0, keepdims=True), axis=1, keepdims=True)
    area_parts = jnp.concatenate(three_parts(wet_area), axis=0)
    adjoint[...] = jnp.zeros_like(adjoint)

    def weigh(w, carry):
        back = lax.dot_general(
            area_parts, tiles[w], (((1,), (1,)), ((), ())), preferred_element_type=jnp.float32
        )
        back = back[:blocks] + back[blocks:2 * blocks] + back[2 * blocks:]
        slot_id = lax.broadcasted_iota(jnp.int32, (slots, blocks), 0)
        takes = jnp.where(inverse_v[pl.ds(w, 1), :] == slot_id, 1.0, 0.0).astype(jnp.bfloat16)
        spread = jnp.dot(
            takes, jnp.concatenate(three_parts(back), axis=1), preferred_element_type=jnp.float32
        )
        adjoint[...] += spread[:, :cells] + spread[:, cells:2 * cells] + spread[:, 2 * cells:]
        return carry

    lax.fori_loop(0, ntiles, weigh, 0)
    to_scalars.wait()

    def weighted(first, acc):
        first = pl.multiple_of(first, cap)
        weights = adjoint[pl.ds(first, cap), :]
        for j in range(cap):
            acc = acc - received[first + j].astype(jnp.float32) * weights[j:j + 1]
        return acc

    acc = weighted(mine, acc)
    for i, (dy, dx) in enumerate(order):
        peer = lax.rem(me_y + ny - dy, ny) * nx + lax.rem(me_x + nx - dx, nx)
        arrived = received.at[pl.ds(peer * cap, cap)]
        pltpu.make_async_copy(arrived, arrived, recv_sem.at[i]).wait()
        acc = weighted(peer * cap, acc)

    lane = lax.broadcasted_iota(jnp.int32, (fields, cells), 1)
    field = lax.broadcasted_iota(jnp.int32, (fields, cells), 0)
    diff = jnp.sum(acc, axis=1, keepdims=True)
    line = jnp.sum(jnp.where(lane == field, diff, 0.0), axis=0, keepdims=True)
    line = line + jnp.where(lane[:1] == fields, wet_sum, 0.0)

    def send_line(line, part, into, n, me, axis, s_sem, r_sem):
        part[0] = line
        into[me] = line
        for step in range(1, n):
            pltpu.make_async_remote_copy(
                src_ref=part.at[0],
                dst_ref=into.at[me],
                send_sem=s_sem,
                recv_sem=r_sem,
                device_id={axis: lax.rem(me + step, n)},
                device_id_type=MESH,
            ).start()

    def sum_lines(into, n, r_sem):
        others = into.at[pl.ds(0, n - 1)]
        pltpu.make_async_copy(others, others, r_sem).wait()
        return jnp.sum(into[...], axis=0)

    chunk_targets = blocks // CHUNKS

    def regrid(chunk, carry):
        base = chunk * chunk_targets
        for t in range(chunk_targets):
            for w in range(ntiles):
                slot = inverse[w, base + t]
                grouped[t * fields:(t + 1) * fields, w * cells:(w + 1) * cells] = received[slot]
        raw = jnp.dot(
            grouped[...], tiles[...].reshape(ntiles * cells, cells),
            preferred_element_type=jnp.float32,
        )
        at = pl.ds(pl.multiple_of(base, chunk_targets), chunk_targets)
        raw_ref[at] = raw.reshape(chunk_targets, fields, cells)
        return carry

    send_line(line, part, rows, n_row, me_row, "row", row_send, row_recv)
    lax.fori_loop(0, CHUNKS // 2, regrid, 0)
    line = sum_lines(rows, n_row, row_recv)
    send_line(line, part_all, cols, n_col, me_col, "col", col_send, col_recv)
    lax.fori_loop(CHUNKS // 2, CHUNKS, regrid, 0)
    line = sum_lines(cols, n_col, col_recv)
    line = jnp.broadcast_to(line, (fields, cells))
    diff = jnp.sum(jnp.where(lane == field, line, 0.0), axis=1, keepdims=True)
    wet_all = jnp.sum(jnp.where(lane == fields, line, 0.0), axis=1, keepdims=True)
    shift_ref[...] = jnp.broadcast_to(diff / jnp.maximum(wet_all, 1.0), (fields, cells))

    whole = received.at[pl.ds(0, slots - cap)]
    pltpu.make_async_copy(whole, whole, send_sem).wait()
    others = rows.at[pl.ds(0, n_row - 1)]
    pltpu.make_async_copy(others, others, row_send).wait()
    others = cols.at[pl.ds(0, n_col - 1)]
    pltpu.make_async_copy(others, others, col_send).wait()


def body(n_row, n_col, air_flux, air_area, sea_area, wet_mask, tiles, send_block, slot, tile):
    steps, blocks, fields, cells = air_flux.shape
    ntiles = tiles.shape[0]
    slots = send_block.shape[1]
    kinds = slot.shape[1]
    vmem = pl.BlockSpec(memory_space=pltpu.VMEM)
    raw, shift = pl.pallas_call(
        functools.partial(kernel, n_row, n_col),
        out_shape=(
            jax.ShapeDtypeStruct((blocks, fields, cells), jnp.float32),
            jax.ShapeDtypeStruct((fields, cells), jnp.float32),
        ),
        in_specs=[pl.BlockSpec(memory_space=pltpu.HBM)] * 8,
        out_specs=(vmem, vmem),
        scratch_shapes=[
            pltpu.SMEM((1, slots), jnp.int32),
            pltpu.VMEM((kinds, blocks), jnp.int32),
            pltpu.VMEM((kinds, blocks), jnp.int32),
            pltpu.VMEM((steps, blocks, fields, cells), jnp.bfloat16),
            pltpu.VMEM((blocks, cells), jnp.float32),
            pltpu.VMEM((blocks, cells), jnp.float32),
            pltpu.VMEM((1, blocks), jnp.int32),
            pltpu.VMEM((ntiles, cells, cells), jnp.bfloat16),
            pltpu.VMEM((ntiles, blocks), jnp.int32),
            pltpu.SMEM((ntiles, blocks), jnp.int32),
            pltpu.VMEM((blocks, fields, cells), jnp.bfloat16),
            pltpu.VMEM((slots, fields, cells), jnp.bfloat16),
            pltpu.VMEM((slots + 1, fields, cells), jnp.bfloat16),
            pltpu.VMEM((blocks // CHUNKS * fields, ntiles * cells), jnp.bfloat16),
            pltpu.VMEM((slots, cells), jnp.float32),
            pltpu.VMEM((1, 1, cells), jnp.float32),
            pltpu.VMEM((n_row, 1, cells), jnp.float32),
            pltpu.VMEM((1, 1, cells), jnp.float32),
            pltpu.VMEM((n_col, 1, cells), jnp.float32),
            pltpu.SemaphoreType.DMA((7,)),
            pltpu.SemaphoreType.DMA((CHUNKS,)),
            pltpu.SemaphoreType.DMA,
            pltpu.SemaphoreType.DMA,
            pltpu.SemaphoreType.DMA((n_col - 1,)),
        ] + [pltpu.SemaphoreType.DMA] * 4,
        compiler_params=pltpu.CompilerParams(
            collective_id=0, has_side_effects=True, vmem_limit_bytes=60 * 1024 * 1024
        ),
    )(
        send_block, slot.T, tile.T, air_flux, air_area, sea_area, wet_mask[None], tiles,
    )
    return wet_mask.astype(jnp.float32)[:, None, None] * (raw + shift[None])


def solution(mesh):
    n_row, n_col = mesh.shape["row"], mesh.shape["col"]
    return jax.shard_map(
        functools.partial(body, n_row, n_col),
        mesh=mesh,
        in_specs=(
            P(None, WIDE, None, None), P(WIDE, None), P(WIDE, None), P(WIDE), P(),
            P(WIDE, None), P(WIDE, None), P(WIDE, None),
        ),
        out_specs=P(WIDE, None, None),
        check_vma=False,
    )
```

time: 67.7 us -> 55.8 us (0.82)
  Pallas kernels: 61.4 us -> 52.6 us
  local copies, waits for them, and re-layouts: 1.49 us -> 0 us
  other arithmetic: 4.5 us -> 3.06 us
    pallas_call x1, Pallas kernels: 61.4 us -> 52.6 us  [body(): pl.pallas_call(functools.partial(kernel, n_row, n_col), out_shape=(jax.Sh...]
    add x2 -> x0, local copies, waits for them, and re-layouts: 0.78 us -> none  [body(): slots + jnp.sum(jnp.where(tile[:, :, None] == ids, slot[:, :, None] - slo...]
    reduce_sum x1 -> x0, other arithmetic: 0.73 us -> none  [body(): jnp.sum(jnp.where(tile[:, :, None] == ids, slot[:, :, None] - slots, 0),...]
    broadcast_in_dim x1 -> x0, local copies, waits for them, and re-layouts: 0.71 us -> none  [body(): wet_wide = jnp.broadcast_to(wet[:, None], (blocks, cells))]
    sub x1 -> x0, other arithmetic: 0.7 us -> none  [body(): slot[:, :, None] - slots]
where the time goes in v2:
time: 55.8 us; the launch traced here: 55.6 us
  Pallas kernels  52.6 us (94%)
  other arithmetic  3.06 us (5%)
    pallas_call x1, Pallas kernels, body(): pl.pallas_call(functools.partial(kernel, n_row, n_col), out_shape=(jax.Sh...  52.6 us
    mul x1, other arithmetic, body(): return wet_mask.astype(jnp.float32)[:, None, None] * (raw + shift[None])  2.4 us

profile of v2, /device:TPU:1, one launch (start us, length us, event | category | flops | bytes accessed | tf_op | source)
XLA Modules:
  0.0 55.6 jit_solution(8086235689942863024)
XLA Ops:
  0.0 0.7 %convert_element_type.3 = f32[128]{0:T(128)S(1)} convert(s32[128]{0:T(128)} %param.11) | non-fusion elementwise | flops 128 | bytes 1024 | tf_op jit(solution)/shard_map/convert_element_type | solution.py:267
  0.7 52.6 %shard_map.82 = (f32[128,16,128]{2,1,0:T(8,128)}, f32[16,128]{1,0:T(8,128)}) custom-call(s32[1,256]{1,0:T(1,128)} %send_ref.1, s32[16,128]{1,0:T(8,128)} %bitcast.3, s32[16,128]{1,0:T(8,128)} %bitcast.4, bf16[4,128,16,128]{3,2,1,0:T(8,128)(2,1)} %air_ref.1, f32[128,128]{1,0:T(8,128)} %air_area_ref.1, f32[128,128]{1,0:T(8,128)} %sea_area_ref.1, ...), custom_call_target="tpu_custom_call" | custom-call | tf_op jit(solution)/shard_map/pallas_call | solution.py:227
  53.2 2.4 %add_multiply_fusion = f32[128,16,128]{2,1,0:T(8,128)} fusion(f32[128,16,128]{2,1,0:T(8,128)} %get-tuple-element.7, f32[16,128]{1,0:T(8,128)} %get-tuple-element.8, f32[128]{0:T(128)S(1)} %convert_element_type.3), kind=kLoop, calls=%fused_computation | loop fusion | flops 524288 | bytes 2105856 | tf_op jit(solution)/shard_map/mul | solution.py:267

commit v3 on v2

--- a/solution.py
+++ b/solution.py
@@ -10,12 +10,15 @@
 MESH = pl.DeviceIdType.MESH
 WIDE = ("row", "col")
 CHUNKS = 4
+TARGET_CHUNKS = 4
 
 
 def peer_order(n_col):
-    ny, nx = (8, 4) if n_col == 32 else (n_col, 1)
+    ny, nx = (8, 4) if n_col == 32 else (n_col // 2, 2)
     ys = sorted(range(ny), key=lambda d: (-min(d, ny - d), d))
-    return ny, nx, [(dy, dx) for dx in range(nx) for dy in ys if (dy, dx) != (0, 0)][::-1]
+    early = [(dy, dx) for dx in range(1, nx) for dy in ys][::-1]
+    late = [(dy, 0) for dy in ys if dy]
+    return ny, nx, early, late
 
 
 def three_parts(x):
@@ -29,16 +32,17 @@
 def kernel(
     n_row, n_col,
     send_ref, slot_ref, tile_ref, air_ref, air_area_ref, sea_area_ref, wet_ref, tiles_ref,
-    raw_ref, shift_ref,
+    raw_ref, shift_ref, wet_out_ref,
     send, slot_of, tile_of, air, air_area, sea_area, wet, tiles,
-    inverse_v, inverse, sent, outbound, received, grouped, adjoint, part, rows, part_all, cols,
-    small_sem, load_sem, inverse_sem, send_sem, recv_sem, row_send, row_recv, col_send, col_recv,
+    inverse_v, inverse, sent, outbound, received, adjoint, returned, part, rows, part_all, cols,
+    small_sem, load_sem, inverse_sem, send_sem, recv_sem, back_send, back_recv,
+    row_send, row_recv, col_send, col_recv,
 ):
     steps, blocks, fields, cells = air.shape
     cap = outbound.shape[0] // n_col
     slots = n_col * cap
     ntiles = tiles.shape[0]
-    ny, nx, order = peer_order(n_col)
+    ny, nx, early, late = peer_order(n_col)
     me_row = lax.axis_index("row")
     me_col = lax.axis_index("col")
     per = blocks // CHUNKS
@@ -99,18 +103,32 @@
     pl.semaphore_wait(barrier, n_col + n_row - 2)
 
     me_y, me_x = me_col // nx, lax.rem(me_col, nx)
-    for i, (dy, dx) in enumerate(order):
-        peer = lax.rem(me_y + dy, ny) * nx + lax.rem(me_x + dx, nx)
-        for j in range(cap):
-            outbound[peer * cap + j] = sent[send[0, peer * cap + j]]
-        pltpu.make_async_remote_copy(
-            src_ref=outbound.at[pl.ds(peer * cap, cap)],
-            dst_ref=received.at[pl.ds(mine, cap)],
-            send_sem=send_sem,
-            recv_sem=recv_sem.at[i],
-            device_id={"col": peer},
-            device_id_type=MESH,
-        ).start()
+
+    def ahead(dy, dx):
+        return lax.rem(me_y + dy, ny) * nx + lax.rem(me_x + dx, nx)
+
+    def behind(dy, dx):
+        return lax.rem(me_y + ny - dy, ny) * nx + lax.rem(me_x + nx - dx, nx)
+
+    def send_blocks(displacements, first):
+        for i, (dy, dx) in enumerate(displacements):
+            peer = ahead(dy, dx)
+            for j in range(cap):
+                outbound[peer * cap + j] = sent[send[0, peer * cap + j]]
+            pltpu.make_async_remote_copy(
+                src_ref=outbound.at[pl.ds(peer * cap, cap)],
+                dst_ref=received.at[pl.ds(mine, cap)],
+                send_sem=send_sem,
+                recv_sem=recv_sem.at[first + i],
+                device_id={"col": peer},
+                device_id_type=MESH,
+            ).start()
+
+    def wait_blocks(displacement, i):
+        arrived = received.at[pl.ds(behind(*displacement) * cap, cap)]
+        pltpu.make_async_copy(arrived, arrived, recv_sem.at[i]).wait()
+
+    send_blocks(early, 0)
     for j in range(cap):
         received[mine + j] = sent[send[0, mine + j]]
     to_scalars = pltpu.make_async_copy(inverse_v, inverse, inverse_sem)
@@ -125,6 +143,7 @@
     wet_wide = jnp.broadcast_to(wet[...].astype(jnp.float32), square)
     wet_column = jnp.sum(jnp.where(on_diagonal, wet_wide, 0.0), axis=1, keepdims=True)
     wet_area = sea_area[...] * wet_column
+    wet_out_ref[...] = jnp.broadcast_to(wet_column, (blocks, cells))
     wet_sum = jnp.sum(jnp.sum(wet_area, axis=0, keepdims=True), axis=1, keepdims=True)
     area_parts = jnp.concatenate(three_parts(wet_area), axis=0)
     adjoint[...] = jnp.zeros_like(adjoint)
@@ -145,19 +164,33 @@
     lax.fori_loop(0, ntiles, weigh, 0)
     to_scalars.wait()
 
-    def weighted(first, acc):
+    for dy, dx in late:
+        source = behind(dy, dx)
+        pltpu.make_async_remote_copy(
+            src_ref=adjoint.at[pl.ds(pl.multiple_of(source * cap, cap), cap)],
+            dst_ref=returned.at[pl.ds(pl.multiple_of(mine, cap), cap)],
+            send_sem=back_send,
+            recv_sem=back_recv,
+            device_id={"col": source},
+            device_id_type=MESH,
+        ).start()
+    send_blocks(late, len(early))
+
+    def weighted(values, weights_ref, first, acc):
         first = pl.multiple_of(first, cap)
-        weights = adjoint[pl.ds(first, cap), :]
+        weights = weights_ref[pl.ds(first, cap), :]
         for j in range(cap):
-            acc = acc - received[first + j].astype(jnp.float32) * weights[j:j + 1]
+            acc = acc - values[first + j].astype(jnp.float32) * weights[j:j + 1]
         return acc
 
-    acc = weighted(mine, acc)
-    for i, (dy, dx) in enumerate(order):
-        peer = lax.rem(me_y + ny - dy, ny) * nx + lax.rem(me_x + nx - dx, nx)
-        arrived = received.at[pl.ds(peer * cap, cap)]
-        pltpu.make_async_copy(arrived, arrived, recv_sem.at[i]).wait()
-        acc = weighted(peer * cap, acc)
+    acc = weighted(received, adjoint, mine, acc)
+    for i, displacement in enumerate(early):
+        wait_blocks(displacement, i)
+        acc = weighted(received, adjoint, behind(*displacement) * cap, acc)
+    backs = returned.at[pl.ds(0, cap * len(late))]
+    pltpu.make_async_copy(backs, backs, back_recv).wait()
+    for displacement in late:
+        acc = weighted(outbound, returned, ahead(*displacement) * cap, acc)
 
     lane = lax.broadcasted_iota(jnp.int32, (fields, cells), 1)
     field = lax.broadcasted_iota(jnp.int32, (fields, cells), 0)
@@ -183,27 +216,31 @@
         pltpu.make_async_copy(others, others, r_sem).wait()
         return jnp.sum(into[...], axis=0)
 
-    chunk_targets = blocks // CHUNKS
-
-    def regrid(chunk, carry):
+    chunk_targets = blocks // TARGET_CHUNKS
+
+    def regrid(chunk):
         base = chunk * chunk_targets
-        for t in range(chunk_targets):
-            for w in range(ntiles):
-                slot = inverse[w, base + t]
-                grouped[t * fields:(t + 1) * fields, w * cells:(w + 1) * cells] = received[slot]
-        raw = jnp.dot(
-            grouped[...], tiles[...].reshape(ntiles * cells, cells),
-            preferred_element_type=jnp.float32,
-        )
-        at = pl.ds(pl.multiple_of(base, chunk_targets), chunk_targets)
-        raw_ref[at] = raw.reshape(chunk_targets, fields, cells)
-        return carry
+        raw = jnp.zeros((chunk_targets * fields, cells), jnp.float32)
+        for w in range(0, ntiles, 2):
+            pairs = [
+                jnp.concatenate(
+                    [received[inverse[w, base + t]], received[inverse[w + 1, base + t]]], axis=1
+                )
+                for t in range(chunk_targets)
+            ]
+            raw = raw + jnp.dot(
+                jnp.concatenate(pairs, axis=0), tiles[w:w + 2].reshape(2 * cells, cells),
+                preferred_element_type=jnp.float32,
+            )
+        raw_ref[base:base + chunk_targets] = raw.reshape(chunk_targets, fields, cells)
 
     send_line(line, part, rows, n_row, me_row, "row", row_send, row_recv)
-    lax.fori_loop(0, CHUNKS // 2, regrid, 0)
     line = sum_lines(rows, n_row, row_recv)
     send_line(line, part_all, cols, n_col, me_col, "col", col_send, col_recv)
-    lax.fori_loop(CHUNKS // 2, CHUNKS, regrid, 0)
+    for i, displacement in enumerate(late):
+        wait_blocks(displacement, len(early) + i)
+    for chunk in range(TARGET_CHUNKS):
+        regrid(chunk)
     line = sum_lines(cols, n_col, col_recv)
     line = jnp.broadcast_to(line, (fields, cells))
     diff = jnp.sum(jnp.where(lane == field, line, 0.0), axis=1, keepdims=True)
@@ -212,6 +249,7 @@
 
     whole = received.at[pl.ds(0, slots - cap)]
     pltpu.make_async_copy(whole, whole, send_sem).wait()
+    pltpu.make_async_copy(backs, backs, back_send).wait()
     others = rows.at[pl.ds(0, n_row - 1)]
     pltpu.make_async_copy(others, others, row_send).wait()
     others = cols.at[pl.ds(0, n_col - 1)]
@@ -224,14 +262,15 @@
     slots = send_block.shape[1]
     kinds = slot.shape[1]
     vmem = pl.BlockSpec(memory_space=pltpu.VMEM)
-    raw, shift = pl.pallas_call(
+    raw, shift, wet = pl.pallas_call(
         functools.partial(kernel, n_row, n_col),
         out_shape=(
-            jax.ShapeDtypeStruct((blocks, fields, cells), jnp.float32),
-            jax.ShapeDtypeStruct((fields, cells), jnp.float32),
+            pltpu.VMEM((blocks, fields, cells), jnp.float32),
+            pltpu.VMEM((fields, cells), jnp.float32),
+            pltpu.VMEM((blocks, cells), jnp.float32),
         ),
         in_specs=[pl.BlockSpec(memory_space=pltpu.HBM)] * 8,
-        out_specs=(vmem, vmem),
+        out_specs=(vmem, vmem, vmem),
         scratch_shapes=[
             pltpu.SMEM((1, slots), jnp.int32),
             pltpu.VMEM((kinds, blocks), jnp.int32),
@@ -246,7 +285,7 @@
             pltpu.VMEM((blocks, fields, cells), jnp.bfloat16),
             pltpu.VMEM((slots, fields, cells), jnp.bfloat16),
             pltpu.VMEM((slots + 1, fields, cells), jnp.bfloat16),
-            pltpu.VMEM((blocks // CHUNKS * fields, ntiles * cells), jnp.bfloat16),
+            pltpu.VMEM((slots, cells), jnp.float32),
             pltpu.VMEM((slots, cells), jnp.float32),
             pltpu.VMEM((1, 1, cells), jnp.float32),
             pltpu.VMEM((n_row, 1, cells), jnp.float32),
@@ -257,14 +296,14 @@
             pltpu.SemaphoreType.DMA,
             pltpu.SemaphoreType.DMA,
             pltpu.SemaphoreType.DMA((n_col - 1,)),
-        ] + [pltpu.SemaphoreType.DMA] * 4,
+        ] + [pltpu.SemaphoreType.DMA] * 6,
         compiler_params=pltpu.CompilerParams(
-            collective_id=0, has_side_effects=True, vmem_limit_bytes=60 * 1024 * 1024
+            collective_id=0, has_side_effects=True, vmem_limit_bytes=55 * 1024 * 1024
         ),
     )(
         send_block, slot.T, tile.T, air_flux, air_area, sea_area, wet_mask[None], tiles,
     )
-    return wet_mask.astype(jnp.float32)[:, None, None] * (raw + shift[None])
+    return wet[:, None, :] * (raw + shift[None])
 
 
 def solution(mesh):

time: 55.8 us -> 50.1 us (0.90)
  Pallas kernels: 52.6 us -> 48.9 us
  other arithmetic: 3.06 us -> 1.09 us
    pallas_call x1, Pallas kernels: 52.6 us -> 48.9 us  [body(): pl.pallas_call(functools.partial(kernel, n_row, n_col), out_shape=(pltpu....]
    mul x1, other arithmetic: 2.4 us -> 1.09 us  [body(): return wet[:, None, :] * (raw + shift[None])]
    convert_element_type x1 -> x0, other arithmetic: 0.66 us -> none  [body(): return wet_mask.astype(jnp.float32)[:, None, None] * (raw + shift[None])]
where the time goes in v3:
time: 50.1 us; the launch traced here: 50 us
  Pallas kernels  48.9 us (98%)
  other arithmetic  1.09 us (2%)
    pallas_call x1, Pallas kernels, body(): pl.pallas_call(functools.partial(kernel, n_row, n_col), out_shape=(pltpu....  48.9 us
    mul x1, other arithmetic, body(): return wet[:, None, :] * (raw + shift[None])  1.09 us

profile of v3, /device:TPU:1, one launch (start us, length us, event | category | flops | bytes accessed | tf_op | source)
XLA Modules:
  0.0 50.0 jit_solution(6416317932087009774)
XLA Ops:
  0.0 48.9 %shard_map.82 = (f32[128,16,128]{2,1,0:T(8,128)S(1)}, f32[16,128]{1,0:T(8,128)S(1)}, f32[128,128]{1,0:T(8,128)S(1)}) custom-call(s32[1,256]{1,0:T(1,128)} %send_ref.1, s32[16,128]{1,0:T(8,128)} %bitcast.3, s32[16,128]{1,0:T(8,128)} %bitcast.4, bf16[4,128,16,128]{3,2,1,0:T(8,128)(2,1)} %air_ref.1, f32[128,128]{1,0:T(8,128)} %air_area_ref.1, ...), custom_call_target="tpu_custom_call" | custom-call | tf_op jit(solution)/shard_map/pallas_call | solution.py:265
  48.9 1.1 %add_multiply_fusion = f32[128,16,128]{2,1,0:T(8,128)} fusion(f32[128,16,128]{2,1,0:T(8,128)S(1)} %get-tuple-element.9, f32[16,128]{1,0:T(8,128)S(1)} %get-tuple-element.10, f32[128,128]{1,0:T(8,128)S(1)} %get-tuple-element.8), kind=kLoop, calls=%fused_computation | loop fusion | flops 524288 | bytes 2170880 | tf_op jit(solution)/shard_map/mul | solution.py:306

commit v4 on v3

--- a/solution.py
+++ b/solution.py
@@ -10,14 +10,17 @@
 MESH = pl.DeviceIdType.MESH
 WIDE = ("row", "col")
 CHUNKS = 4
+TILES_A_STEP = 8
+HELD = 23
 TARGET_CHUNKS = 4
 
 
 def peer_order(n_col):
     ny, nx = (8, 4) if n_col == 32 else (n_col // 2, 2)
     ys = sorted(range(ny), key=lambda d: (-min(d, ny - d), d))
-    early = [(dy, dx) for dx in range(1, nx) for dy in ys][::-1]
-    late = [(dy, 0) for dy in ys if dy]
+    every = [(dy, dx) for dx in range(nx) for dy in ys if (dy, dx) != (0, 0)]
+    late = [(dy, dx) for dy, dx in every if dx == 0]
+    early = [place for place in every[::-1] if place not in late]
     return ny, nx, early, late
 
 
@@ -148,21 +151,31 @@
     area_parts = jnp.concatenate(three_parts(wet_area), axis=0)
     adjoint[...] = jnp.zeros_like(adjoint)
 
-    def weigh(w, carry):
+    slot_id = lax.broadcasted_iota(jnp.int32, (slots, blocks), 0)
+
+    def weigh(step, carry):
+        first_tile = step * TILES_A_STEP
         back = lax.dot_general(
-            area_parts, tiles[w], (((1,), (1,)), ((), ())), preferred_element_type=jnp.float32
+            area_parts,
+            tiles[pl.ds(first_tile, TILES_A_STEP)].reshape(TILES_A_STEP * cells, cells),
+            (((1,), (1,)), ((), ())), preferred_element_type=jnp.float32,
         )
         back = back[:blocks] + back[blocks:2 * blocks] + back[2 * blocks:]
-        slot_id = lax.broadcasted_iota(jnp.int32, (slots, blocks), 0)
-        takes = jnp.where(inverse_v[pl.ds(w, 1), :] == slot_id, 1.0, 0.0).astype(jnp.bfloat16)
+        takes, parts = [], []
+        for w in range(TILES_A_STEP):
+            taken = inverse_v[pl.ds(first_tile + w, 1), :]
+            takes.append(jnp.where(taken == slot_id, 1.0, 0.0).astype(jnp.bfloat16))
+            parts.append(
+                jnp.concatenate(three_parts(back[:, w * cells:(w + 1) * cells]), axis=1)
+            )
         spread = jnp.dot(
-            takes, jnp.concatenate(three_parts(back), axis=1), preferred_element_type=jnp.float32
+            jnp.concatenate(takes, axis=1), jnp.concatenate(parts, axis=0),
+            preferred_element_type=jnp.float32,
         )
         adjoint[...] += spread[:, :cells] + spread[:, cells:2 * cells] + spread[:, 2 * cells:]
         return carry
 
-    lax.fori_loop(0, ntiles, weigh, 0)
-    to_scalars.wait()
+    lax.fori_loop(0, ntiles // TILES_A_STEP, weigh, 0)
 
     for dy, dx in late:
         source = behind(dy, dx)
@@ -174,7 +187,6 @@
             device_id={"col": source},
             device_id_type=MESH,
         ).start()
-    send_blocks(late, len(early))
 
     def weighted(values, weights_ref, first, acc):
         first = pl.multiple_of(first, cap)
@@ -185,6 +197,8 @@
 
     acc = weighted(received, adjoint, mine, acc)
     for i, displacement in enumerate(early):
+        if i == HELD * len(early) // 24:
+            send_blocks(late, len(early))
         wait_blocks(displacement, i)
         acc = weighted(received, adjoint, behind(*displacement) * cap, acc)
     backs = returned.at[pl.ds(0, cap * len(late))]
@@ -239,6 +253,7 @@
     send_line(line, part_all, cols, n_col, me_col, "col", col_send, col_recv)
     for i, displacement in enumerate(late):
         wait_blocks(displacement, len(early) + i)
+    to_scalars.wait()
     for chunk in range(TARGET_CHUNKS):
         regrid(chunk)
     line = sum_lines(cols, n_col, col_recv)

time: 50.1 us -> 49.7 us (level)
  no operation moved by 1% of the time
where the time goes in v4:
time: 49.7 us; the launch traced here: 49.6 us
  Pallas kernels  48.5 us (98%)
  other arithmetic  1.09 us (2%)
    pallas_call x1, Pallas kernels, body(): pl.pallas_call(functools.partial(kernel, n_row, n_col), out_shape=(pltpu....  48.5 us
    mul x1, other arithmetic, body(): return wet[:, None, :] * (raw + shift[None])  1.09 us

profile of v4, /device:TPU:1, one launch (start us, length us, event | category | flops | bytes accessed | tf_op | source)
XLA Modules:
  0.0 49.6 jit_solution(112139068318229334)
XLA Ops:
  0.0 48.5 %shard_map.82 = (f32[128,16,128]{2,1,0:T(8,128)S(1)}, f32[16,128]{1,0:T(8,128)S(1)}, f32[128,128]{1,0:T(8,128)S(1)}) custom-call(s32[1,256]{1,0:T(1,128)} %send_ref.1, s32[16,128]{1,0:T(8,128)} %bitcast.3, s32[16,128]{1,0:T(8,128)} %bitcast.4, bf16[4,128,16,128]{3,2,1,0:T(8,128)(2,1)} %air_ref.1, f32[128,128]{1,0:T(8,128)} %air_area_ref.1, ...), custom_call_target="tpu_custom_call" | custom-call | tf_op jit(solution)/shard_map/pallas_call | solution.py:280
  48.5 1.1 %add_multiply_fusion = f32[128,16,128]{2,1,0:T(8,128)} fusion(f32[128,16,128]{2,1,0:T(8,128)S(1)} %get-tuple-element.9, f32[16,128]{1,0:T(8,128)S(1)} %get-tuple-element.10, f32[128,128]{1,0:T(8,128)S(1)} %get-tuple-element.8), kind=kLoop, calls=%fused_computation | loop fusion | flops 524288 | bytes 2170880 | tf_op jit(solution)/shard_map/mul | solution.py:321

commit v5 on v4

--- a/solution.py
+++ b/solution.py
@@ -19,7 +19,7 @@
     ny, nx = (8, 4) if n_col == 32 else (n_col // 2, 2)
     ys = sorted(range(ny), key=lambda d: (-min(d, ny - d), d))
     every = [(dy, dx) for dx in range(nx) for dy in ys if (dy, dx) != (0, 0)]
-    late = [(dy, dx) for dy, dx in every if dx == 0]
+    late = [(dy, dx) for dy, dx in every[::-1] if dx == 0]
     early = [place for place in every[::-1] if place not in late]
     return ny, nx, early, late
 

time: 49.7 us -> 49.1 us (0.988)
  Pallas kernels: 48.5 us -> 47.9 us
    pallas_call x1, Pallas kernels: 48.5 us -> 47.9 us  [body(): pl.pallas_call(functools.partial(kernel, n_row, n_col), out_shape=(pltpu....]
where the time goes in v5:
time: 49.1 us; the launch traced here: 49 us
  Pallas kernels  47.9 us (98%)
  other arithmetic  1.09 us (2%)
    pallas_call x1, Pallas kernels, body(): pl.pallas_call(functools.partial(kernel, n_row, n_col), out_shape=(pltpu....  47.9 us
    mul x1, other arithmetic, body(): return wet[:, None, :] * (raw + shift[None])  1.09 us

profile of v5, /device:TPU:1, one launch (start us, length us, event | category | flops | bytes accessed | tf_op | source)
XLA Modules:
  0.0 49.0 jit_solution(7803146467833854823)
XLA Ops:
  0.0 47.9 %shard_map.82 = (f32[128,16,128]{2,1,0:T(8,128)S(1)}, f32[16,128]{1,0:T(8,128)S(1)}, f32[128,128]{1,0:T(8,128)S(1)}) custom-call(s32[1,256]{1,0:T(1,128)} %send_ref.1, s32[16,128]{1,0:T(8,128)} %bitcast.3, s32[16,128]{1,0:T(8,128)} %bitcast.4, bf16[4,128,16,128]{3,2,1,0:T(8,128)(2,1)} %air_ref.1, f32[128,128]{1,0:T(8,128)} %air_area_ref.1, ...), custom_call_target="tpu_custom_call" | custom-call | tf_op jit(solution)/shard_map/pallas_call | solution.py:280
  47.9 1.1 %add_multiply_fusion = f32[128,16,128]{2,1,0:T(8,128)} fusion(f32[128,16,128]{2,1,0:T(8,128)S(1)} %get-tuple-element.9, f32[16,128]{1,0:T(8,128)S(1)} %get-tuple-element.10, f32[128,128]{1,0:T(8,128)S(1)} %get-tuple-element.8), kind=kLoop, calls=%fused_computation | loop fusion | flops 524288 | bytes 2170880 | tf_op jit(solution)/shard_map/mul | solution.py:321
